TPU v7x, 8 devices: a whole 2x2x1 slice. The times are simulated.
8 devices in a mesh: rep: 2 (over y, z), dp: 4 (over x, core).
Axes of the slice: x: 2, y: 2, z: 1, core: 2. Of those that a mesh axis runs over, the one named last changes fastest.
Arguments:
- x: bfloat16 [8, 2048, 1280], P(('rep', 'dp')), parts along dimension 0
- dy: bfloat16 [8, 2048, 1280], P(('rep', 'dp')), parts along dimension 0
- w_gate: bfloat16 [2, 1280, 4096], P(None, 'dp')
- w_up: bfloat16 [2, 1280, 4096], P(None, 'dp')
- w_down: bfloat16 [2, 4096, 1280], P(None, 'dp')
Outputs:
- output 1: bfloat16 [8, 2048, 1280], P(('rep', 'dp')), parts along dimension 0
- output 2: bfloat16 [4, 1280, 4096], P('rep', 'dp'), parts along dimension 0
- output 3: bfloat16 [4, 1280, 4096], P('rep', 'dp'), parts along dimension 0
- output 4: bfloat16 [4, 4096, 1280], P('rep', 'dp'), parts along dimension 0
There are 2 independent parts. A program takes and returns all parts, laid end to end along the dimension named above; an argument that names none is the same for every part.
All inputs are finite; a program needn't handle non-finite values.
Results may differ from a plain program's by a relative error of at most 0.018.
Values are sent between devices in bfloat16 or wider.
A program may use at most 2 GiB of HBM per device.

v0:
```python
import jax
import jax.numpy as jnp
from jax import lax

NAMES = ("w_gate", "w_up", "w_down")


def matmul(a, w):
    return jnp.dot(a, w, preferred_element_type=jnp.float32).astype(jnp.bfloat16)


def normed(h):
    wide = h.astype(jnp.float32)
    scale = lax.rsqrt(jnp.mean(wide**2, -1, keepdims=True) + 1e-6)
    return (wide * scale).astype(jnp.bfloat16)


def layer(h, w):
    a = normed(h)
    gate = jnp.dot(a, w["w_gate"], preferred_element_type=jnp.float32)
    up = jnp.dot(a, w["w_up"], preferred_element_type=jnp.float32)
    return h + matmul((jax.nn.silu(gate) * up).astype(jnp.bfloat16), w["w_down"])


def stack(weights, h):
    for number in range(weights["w_gate"].shape[0]):
        h = layer(h, {name: w[number] for name, w in weights.items()})
    return h


def solution(mesh):
    groups = mesh.shape["rep"]

    def step(x, dy, *weights):
        shape = x.shape
        x, dy = (t.reshape(groups, -1, *t.shape[1:]) for t in (x, dy))

        def of_a_group(x, dy):
            _, back = jax.vjp(stack, dict(zip(NAMES, weights, strict=True)), x)
            by_weights, by_x = back(dy)
            return (by_x, *(by_weights[name] for name in NAMES))

        by_x, *by_weights = jax.vmap(of_a_group)(x, dy)
        return (by_x.reshape(shape), *(t.reshape(-1, *t.shape[2:]) for t in by_weights))

    return step
```

profile of v0, /device:TPU:0, one launch (start us, length us, event | category | flops | bytes accessed | tf_op | source)
XLA Modules:
  0.0 1486.3 jit_solution(15536241280664243850)
XLA Ops:
  45.5 38.1 %all-gather.30.cloned.1.call-done = bf16[1,1280,4096]{2,1,0:T(8,128)(2,1)} async-done(((bf16[1,320,4096]{2,1,0:T(8,128)(2,1)}), bf16[1,1280,4096]{2,1,0:T(8,128)(2,1)}) %all-gather.30.cloned.1.call-update) | async-done | bytes 10485776 | tf_op jit(solution)/vmap(jvp())/squeeze | solution.py:27
  83.5 29.2 %fusion.64 = f32[2048,4096]{1,0:T(8,128)} fusion(bf16[1,1280,4096]{2,1,0:T(8,128)(2,1)} %all-gather.30.cloned.1.call-done, bf16[1,2048,1280]{2,1,0:T(8,128)(2,1)} %param.1, f32[2048]{0:T(1024)S(1)} %get-tuple-element.13), kind=kOutput, calls=%fused_computation.86 | convolution fusion | flops 21482700800 | bytes 49291264 | tf_op jit(solution)/vmap(jvp())/dot_general | solution.py:20
  112.7 40.8 %all-gather.32.cloned.1.call-done = bf16[1,1280,4096]{2,1,0:T(8,128)(2,1)} async-done(((bf16[1,320,4096]{2,1,0:T(8,128)(2,1)}), bf16[1,1280,4096]{2,1,0:T(8,128)(2,1)}) %all-gather.32.cloned.1.call-update) | async-done | bytes 10485776 | tf_op jit(solution)/vmap(jvp())/squeeze | solution.py:27
  153.5 29.1 %fusion.60 = f32[2048,4096]{1,0:T(8,128)} fusion(bf16[1,1280,4096]{2,1,0:T(8,128)(2,1)} %all-gather.32.cloned.1.call-done, bf16[1,2048,1280]{2,1,0:T(8,128)(2,1)} %param.1, f32[2048]{0:T(1024)S(1)} %get-tuple-element.13), kind=kOutput, calls=%fused_computation.82 | convolution fusion | flops 21482700800 | bytes 49291264 | tf_op jit(solution)/vmap(jvp())/dot_general | solution.py:21
  182.7 27.6 %fusion.30 = bf16[2048,4096]{1,0:T(8,128)(2,1)} fusion(f32[2048,4096]{1,0:T(8,128)} %fusion.60, f32[2048,4096]{1,0:T(8,128)} %fusion.64), kind=kLoop, calls=%fused_computation.44 | loop fusion | flops 50331648 | bytes 83886080
  210.3 12.7 all-gather.34.cloned.1.call-done
  222.9 30.2 %fusion.45 = (f32[2048]{0:T(1024)S(1)}, bf16[1,1,2048,1280]{2,3,1,0:T(8,128)(2,1)}) fusion(bf16[2048,4096]{1,0:T(8,128)(2,1)} %fusion.30, bf16[1,4096,1280]{2,1,0:T(8,128)(2,1)} %all-gather.34.cloned.1.call-done, bf16[1,2048,1280]{1,2,0:T(8,128)(2,1)} %copy.1), kind=kOutput, calls=%fused_computation.67 | convolution fusion | flops 21487941632 | bytes 37756928 | tf_op jit(solution)/vmap(jvp())/dot_general | solution.py:9
  253.8 38.4 %all-gather.36.cloned.1.call-done = bf16[1,1280,4096]{2,1,0:T(8,128)(2,1)} async-done(((bf16[1,320,4096]{2,1,0:T(8,128)(2,1)}), bf16[1,1280,4096]{2,1,0:T(8,128)(2,1)}) %all-gather.36.cloned.1.call-update) | async-done | bytes 10485776 | tf_op jit(solution)/vmap(jvp())/squeeze | solution.py:27
  292.2 29.2 %fusion.54 = f32[2048,4096]{1,0:T(8,128)} fusion(bf16[1,1280,4096]{2,1,0:T(8,128)(2,1)} %all-gather.36.cloned.1.call-done, bf16[1,1,2048,1280]{2,3,1,0:T(8,128)(2,1)} %get-tuple-element.15, f32[2048]{0:T(1024)S(1)} %bitcast.309), kind=kOutput, calls=%fused_computation.76 | convolution fusion | flops 21482700800 | bytes 49291264 | tf_op jit(solution)/vmap(jvp())/dot_general | solution.py:20
  321.4 40.6 %all-gather.40.cloned.1.call-done = bf16[1,1280,4096]{2,1,0:T(8,128)(2,1)} async-done(((bf16[1,320,4096]{2,1,0:T(8,128)(2,1)}), bf16[1,1280,4096]{2,1,0:T(8,128)(2,1)}) %all-gather.40.cloned.1.call-update) | async-done | bytes 10485776 | tf_op jit(solution)/vmap(jvp())/squeeze | solution.py:27
  362.0 29.6 %fusion.48 = f32[2048,4096]{1,0:T(8,128)} fusion(bf16[1,1280,4096]{2,1,0:T(8,128)(2,1)} %all-gather.40.cloned.1.call-done, bf16[1,1,2048,1280]{2,3,1,0:T(8,128)(2,1)} %get-tuple-element.15, f32[2048]{0:T(1024)S(1)} %bitcast.310), kind=kOutput, calls=%fused_computation.70 | convolution fusion | flops 21482700800 | bytes 49291264 | tf_op jit(solution)/vmap(jvp())/dot_general | solution.py:21
  391.6 39.7 %all-gather.38.cloned.1.call-done = bf16[1,4096,1280]{2,1,0:T(8,128)(2,1)} async-done(((bf16[1,1024,1280]{2,1,0:T(8,128)(2,1)}), bf16[1,4096,1280]{2,1,0:T(8,128)(2,1)}) %all-gather.38.cloned.1.call-update) | async-done | bytes 10485776 | tf_op jit(solution)/vmap(jvp())/squeeze | solution.py:27
  431.2 28.8 %convolution_convert_fusion.1 = bf16[2048,4096]{1,0:T(8,128)(2,1)} fusion(bf16[1,4096,1280]{2,1,0:T(8,128)(2,1)} %all-gather.38.cloned.1.call-done, bf16[1,2048,1280]{2,1,0:T(8,128)(2,1)} %param), kind=kOutput, calls=%fused_computation.54 | convolution fusion | flops 21483225088 | bytes 32505856 | tf_op jit(solution)/vmap(transpose(jvp()))/dot_general | solution.py:9
  460.1 27.1 %fusion.4 = bf16[2048,4096]{1,0:T(8,128)(2,1)S(1)} fusion(f32[2048,4096]{1,0:T(8,128)} %fusion.54, f32[2048,4096]{1,0:T(8,128)} %fusion.48, bf16[2048,4096]{1,0:T(8,128)(2,1)} %convolution_convert_fusion.1), kind=kLoop, calls=%fused_computation.10 | loop fusion | flops 100663296 | bytes 100663296
  492.9 25.4 %fusion.72 = bf16[2048,1280]{0,1:T(8,128)(2,1)} fusion(bf16[2048,4096]{1,0:T(8,128)(2,1)S(1)} %fusion.4, bf16[1,1280,4096]{2,1,0:T(8,128)(2,1)} %all-gather.36.cloned.1.call-done), kind=kOutput, calls=%fused_computation.90 | convolution fusion | flops 21474836480 | bytes 32505856 | tf_op jit(solution)/vmap(transpose(jvp()))/dot_general | solution.py:20
  518.3 37.2 %fusion.47 = (f32[2048]{0:T(1024)S(1)}, bf16[1,1,2048,1280]{2,3,1,0:T(8,128)(2,1)}) fusion(bf16[1,1,2048,1280]{2,3,1,0:T(8,128)(2,1)} %get-tuple-element.15, bf16[2048,1280]{0,1:T(8,128)(2,1)} %fusion.72, bf16[1,1280,4096]{2,1,0:T(8,128)(2,1)} %all-gather.40.cloned.1.call-done, bf16[2048,4096]{1,0:T(8,128)(2,1)} %convolution_convert_fusion.1, ...), kind=kOutput, calls=%fused_computation.69 | convolution fusion | flops 21540894720 | bytes 76554240 | tf_op jit(solution)/vmap(transpose(jvp()))/dot_general | solution.py:21
  555.6 12.4 fusion.115
  568.0 28.9 %convolution_bitcast_fusion = f32[1,4096,1280]{2,1,0:T(8,128)} fusion(bf16[2048,4096]{1,0:T(8,128)(2,1)} %fusion.30, bf16[1,1,2048,1280]{2,3,1,0:T(8,128)(2,1)} %fusion.115), kind=kOutput, calls=%fused_computation.40 | convolution fusion | flops 21474836480 | bytes 42991616 | tf_op jit(solution)/vmap(transpose(jvp()))/dot_general | solution.py:9
  596.9 37.3 %convolution_bitcast_fusion.1 = f32[1,4096,1280]{2,1,0:T(8,128)} fusion(f32[2048,4096]{1,0:T(8,128)} %fusion.48, f32[2048,4096]{1,0:T(8,128)} %fusion.54, bf16[1,2048,1280]{2,1,0:T(8,128)(2,1)} %param), kind=kOutput, calls=%fused_computation.41 | convolution fusion | flops 21525168128 | bytes 93323264 | tf_op jit(solution)/vmap(transpose(jvp()))/dot_general | solution.py:9
  634.4 32.8 %fusion.24 = f32[1,1280,4096]{2,1,0:T(8,128)} fusion(bf16[2048,4096]{1,0:T(8,128)(2,1)} %convolution_convert_fusion.1, f32[2048,4096]{1,0:T(8,128)} %fusion.54, bf16[1,1,2048,1280]{2,3,1,0:T(8,128)(2,1)} %get-tuple-element.15, f32[2048]{0:T(1024)S(1)} %bitcast.312), kind=kOutput, calls=%fused_computation.38 | convolution fusion | flops 21533032448 | bytes 76554240 | tf_op jit(solution)/vmap(transpose(jvp()))/dot_general | solution.py:21
  667.3 29.2 %convolution_convert_fusion = bf16[2048,4096]{1,0:T(8,128)(2,1)} fusion(bf16[1,4096,1280]{2,1,0:T(8,128)(2,1)} %all-gather.34.cloned.1.call-done, bf16[1,1,2048,1280]{2,3,1,0:T(8,128)(2,1)} %fusion.115), kind=kOutput, calls=%fused_computation.53 | convolution fusion | flops 21483225088 | bytes 32505856 | tf_op jit(solution)/vmap(transpose(jvp()))/dot_general | solution.py:9
  696.5 27.1 %fusion.7 = bf16[2048,4096]{1,0:T(8,128)(2,1)S(1)} fusion(f32[2048,4096]{1,0:T(8,128)} %fusion.64, f32[2048,4096]{1,0:T(8,128)} %fusion.60, bf16[2048,4096]{1,0:T(8,128)(2,1)} %convolution_convert_fusion), kind=kLoop, calls=%fused_computation.13 | loop fusion | flops 100663296 | bytes 100663296
  729.4 25.5 %fusion.69 = bf16[2048,1280]{0,1:T(8,128)(2,1)} fusion(bf16[2048,4096]{1,0:T(8,128)(2,1)S(1)} %fusion.7, bf16[1,1280,4096]{2,1,0:T(8,128)(2,1)} %all-gather.30.cloned.1.call-done), kind=kOutput, calls=%fused_computation.89 | convolution fusion | flops 21474836480 | bytes 32505856 | tf_op jit(solution)/vmap(transpose(jvp()))/dot_general | solution.py:20
  754.8 36.9 %fusion.43 = (f32[2048]{0:T(1024)S(1)}, bf16[1,1,2048,1280]{2,3,1,0:T(8,128)(2,1)}) fusion(bf16[1,2048,1280]{1,2,0:T(8,128)(2,1)} %copy.1, bf16[2048,1280]{0,1:T(8,128)(2,1)} %fusion.69, bf16[1,1280,4096]{2,1,0:T(8,128)(2,1)} %all-gather.32.cloned.1.call-done, bf16[2048,4096]{1,0:T(8,128)(2,1)} %convolution_convert_fusion, f32[2048,4096]{1,0:T(8,128)} %fusion.64), kind=kOutput, calls=%fused_computation.65 | convolution fusion | flops 21540894720 | bytes 76554240 | tf_op jit(solution)/vmap(transpose(jvp()))/dot_general | solution.py:21
  792.4 32.8 %fusion.27 = f32[1,1280,4096]{2,1,0:T(8,128)} fusion(bf16[2048,4096]{1,0:T(8,128)(2,1)} %convolution_convert_fusion, f32[2048,4096]{1,0:T(8,128)} %fusion.64, bf16[1,2048,1280]{1,2,0:T(8,128)(2,1)} %copy.1, f32[2048]{0:T(1024)S(1)} %bitcast.314), kind=kOutput, calls=%fused_computation.39 | convolution fusion | flops 21533032448 | bytes 76554240 | tf_op jit(solution)/vmap(transpose(jvp()))/dot_general | solution.py:21
  825.8 28.5 %convolution_bitcast_fusion.3 = f32[1,1280,4096]{2,1,0:T(8,128)} fusion(bf16[2048,4096]{1,0:T(8,128)(2,1)} %copy-done, bf16[1,1,2048,1280]{2,3,1,0:T(8,128)(2,1)} %get-tuple-element.15, f32[2048]{0:T(1024)S(1)} %bitcast.313), kind=kOutput, calls=%fused_computation.43 | convolution fusion | flops 21482700800 | bytes 42999808 | tf_op jit(solution)/vmap(transpose(jvp()))/dot_general | solution.py:20
  854.4 28.7 %convolution_bitcast_fusion.2 = f32[1,1280,4096]{2,1,0:T(8,128)} fusion(bf16[2048,4096]{1,0:T(8,128)(2,1)} %copy-done.1, bf16[1,2048,1280]{1,2,0:T(8,128)(2,1)} %copy.1, f32[2048]{0:T(1024)S(1)} %bitcast.315), kind=kOutput, calls=%fused_computation.42 | convolution fusion | flops 21482700800 | bytes 42999808 | tf_op jit(solution)/vmap(transpose(jvp()))/dot_general | solution.py:20
  883.8 12.4 fusion.114
  912.3 122.0 %reduce-scatter.23.cloned.1.call-done = f32[1,320,4096]{2,1,0:T(8,128)} async-done(((f32[1,1280,4096]{2,1,0:T(8,128)}), f32[1,320,4096]{2,1,0:T(8,128)}) %reduce-scatter.23.cloned.1.call-update) | async-done | bytes 5242896
  1037.1 143.6 %reduce-scatter.25.cloned.1.call-done = f32[1,320,4096]{2,1,0:T(8,128)} async-done(((f32[1,1280,4096]{2,1,0:T(8,128)}), f32[1,320,4096]{2,1,0:T(8,128)}) %reduce-scatter.25.cloned.1.call-update) | async-done | bytes 5242896
  1186.2 141.0 %reduce-scatter.19.cloned.1.call-done = f32[1,320,4096]{2,1,0:T(8,128)} async-done(((f32[1,1280,4096]{2,1,0:T(8,128)}), f32[1,320,4096]{2,1,0:T(8,128)}) %reduce-scatter.19.cloned.1.call-update) | async-done | bytes 5242896
  1330.1 143.6 %reduce-scatter.21.cloned.1.call-done = f32[1,320,4096]{2,1,0:T(8,128)} async-done(((f32[1,1280,4096]{2,1,0:T(8,128)}), f32[1,320,4096]{2,1,0:T(8,128)}) %reduce-scatter.21.cloned.1.call-update) | async-done | bytes 5242896
  (65 shorter events, 85.4 us)
Async XLA Ops:
  7.2 76.4 %all-gather.30.cloned.1.call-start = ((), (), s32[]{:S(2)}) async-start(), calls=%async_computation.6 | async-start | bytes 13107200 | tf_op jit(solution)/vmap(jvp())/squeeze | solution.py:27
  12.7 140.8 %all-gather.32.cloned.1.call-start = ((), (), s32[]{:S(2)}) async-start(), calls=%async_computation.7 | async-start | bytes 13107200 | tf_op jit(solution)/vmap(jvp())/squeeze | solution.py:27
  18.3 204.6 %all-gather.34.cloned.1.call-start = ((), (), s32[]{:S(2)}) async-start(), calls=%async_computation.8 | async-start | bytes 13107200 | tf_op jit(solution)/vmap(jvp())/squeeze | solution.py:27
  23.6 268.6 %all-gather.36.cloned.1.call-start = ((), (), s32[]{:S(2)}) async-start(), calls=%async_computation.9 | async-start | bytes 13107200 | tf_op jit(solution)/vmap(jvp())/squeeze | solution.py:27
  24.2 337.8 %all-gather.40.cloned.1.call-start = ((), (), s32[]{:S(2)}) async-start(), calls=%async_computation.11 | async-start | bytes 13107200 | tf_op jit(solution)/vmap(jvp())/squeeze | solution.py:27
  24.7 406.5 %all-gather.38.cloned.1.call-start = ((), (), s32[]{:S(2)}) async-start(), calls=%async_computation.10 | async-start | bytes 13107200 | tf_op jit(solution)/vmap(jvp())/squeeze | solution.py:27
  25.3 878.7 %reduce-scatter.29.cloned.1.call-start = ((), (), s32[]{:S(2)}) async-start(), calls=%async_computation.17 | async-start | bytes 26214400
  253.1 0.6 copy-start.2
  253.8 108.2 %copy-start.4 = (f32[1,1,2048]{2,1,0:T(1,128)}, f32[1,1,2048]{2,1,0:T(1,128)S(1)}, u32[]{:S(2)}) copy-start(f32[1,1,2048]{2,1,0:T(1,128)S(1)} %rsqrt.23) | copy-start | bytes 24580
  487.2 5.7 copy-start
  518.3 37.2 %copy-start.3 = (f32[2048]{0:T(1024)S(1)}, f32[2048]{0:T(1024)}, u32[]{:S(2)}) copy-start(f32[2048]{0:T(1024)} %copy-done.2) | copy-start | bytes 24580
  518.3 37.3 %copy-start.5 = (f32[1,1,2048]{2,1,0:T(1,128)S(1)}, f32[1,1,2048]{2,1,0:T(1,128)}, u32[]{:S(2)}) copy-start(f32[1,1,2048]{2,1,0:T(1,128)} %copy-done.4) | copy-start | bytes 24580
  596.9 309.9 %reduce-scatter.27.cloned.1.call-start = ((), (), s32[]{:S(2)}) async-start(), calls=%async_computation.16 | async-start | bytes 26214400
  634.3 399.9 %reduce-scatter.23.cloned.1.call-start = ((), (), s32[]{:S(2)}) async-start(), calls=%async_computation.14 | async-start | bytes 26214400
  667.2 513.4 %reduce-scatter.25.cloned.1.call-start = ((), (), s32[]{:S(2)}) async-start(), calls=%async_computation.15 | async-start | bytes 26214400
  723.6 5.7 copy-start.1
  754.8 36.9 %copy-start.8 = (f32[2048]{0:T(1024)S(1)}, f32[2048]{0:T(1024)}, u32[]{:S(2)}) copy-start(f32[2048]{0:T(1024)} %get-tuple-element.12) | copy-start | bytes 24580
  825.1 0.7 copy-start.6
  825.2 502.1 %reduce-scatter.19.cloned.1.call-start = ((), (), s32[]{:S(2)}) async-start(), calls=%async_computation.12 | async-start | bytes 26214400
  854.4 619.3 %reduce-scatter.21.cloned.1.call-start = ((), (), s32[]{:S(2)}) async-start(), calls=%async_computation.13 | async-start | bytes 26214400
  883.1 0.7 copy-start.7
Sparse Core Ops, SparseCore 0:
  12.8 70.6 all-gather.29
  85.6 67.8 all-gather.31
  155.0 67.8 all-gather.33
  224.3 67.8 all-gather.35
  294.1 67.8 all-gather.39
  363.4 67.8 all-gather.37
  597.0 143.9 reduce-scatter.28
  743.6 144.0 reduce-scatter.26
  890.2 143.9 reduce-scatter.22
  1036.6 143.9 reduce-scatter.24
  1183.2 143.9 reduce-scatter.18
  1329.7 143.9 reduce-scatter.20
where the time goes:
time: 1490 us
  waiting for transfers between devices  762 us (51%)
  matrix products  519 us (35%)
  other arithmetic  136 us (9%)
  local copies, waits for them, and re-layouts  53.4 us (4%)
    unnamed x18, waiting for transfers between devices  552 us
    squeeze x6, waiting for transfers between devices, stack(): h = layer(h, {name: w[number] for name, w in weights.items()})  210 us
    dot_general x6, matrix products, layer(): up = jnp.dot(a, w['w_up'], preferred_element_type=jnp.float32)  198 us
    dot_general x6, matrix products, layer(): gate = jnp.dot(a, w['w_gate'], preferred_element_type=jnp.float32)  166 us
    dot_general x5, matrix products, matmul(): jnp.dot(a, w, preferred_element_type=jnp.float32).astype(jnp.bfloat16)  154 us
    unnamed x3, other arithmetic  81.8 us
    unnamed x21, local copies, waits for them, and re-layouts  37.2 us
  transfers between devices with their start and end apart: 12, of which 10 were waited for; matrix products, arithmetic and copies ran while one was open for 35% of the time, Pallas kernels for 0%

commit v1 on v0

v1 whole, which is shorter than its diff:
```python
import jax
import jax.numpy as jnp
from jax import lax
from jax.experimental import pallas as pl
from jax.experimental.pallas import tpu as pltpu
from jax.sharding import PartitionSpec as P

F32, BF16 = jnp.float32, jnp.bfloat16
AXES = ("rep", "dp")
TOKENS, D, FF, LAYERS = 2048, 1280, 4096, 2
DB, FB = D // 4, FF // 4
NN, NT = (((1,), (0,)), ((), ())), (((1,), (1,)), ((), ()))
MESH = pl.DeviceIdType.MESH
TM, TN = 512, 512


def dot(a, b, dims=NN):
    return lax.dot_general(a, b, dims, preferred_element_type=F32)


def pipe(body, grid, ins, outs, *refs):
    def step(at, *blocks):
        body(at.index, *blocks)

    pltpu.emit_pipeline(step, grid=grid, in_specs=ins, out_specs=outs, _explicit_indices=True)(*refs)


def place():
    r, d = lax.axis_index("rep"), lax.axis_index("dp")
    return r, d, d // 2, d % 2


def greet(devices):
    barrier = pltpu.get_barrier_semaphore()
    for device in devices:
        pl.semaphore_signal(barrier, inc=1, device_id=device, device_id_type=MESH)
    pl.semaphore_wait(barrier, len(devices))


def inverse(wide):
    return lax.rsqrt(jnp.mean(wide * wide, -1, keepdims=True) + 1e-6)


STRIPS = 4
CHUNKS = []
for _l in range(LAYERS):
    CHUNKS += [(_l, m, s) for s in range(STRIPS) for m in (0, 1)] + [(_l, 2, s) for s in range(STRIPS)]


def forward_kernel(x, dy, wg, wu, wd, fg, fu, fd, dy_t, a0_t, gate0, up0, mid0, h1, a1_t, gate1, up1, mid1, a, acc, own_send, own_recv, send, recv):
    r, d, chip, core = place()
    across, beside = (1 - chip) * 2 + core, chip * 2 + 1 - core
    over_x, over_y, over_chip = (r, across), (1 - r, d), (r, beside)
    shards, fulls = (wg, wu, wd), (fg, fu, fd)

    def region(chunk, block, half):
        l, m, s = chunk
        if m < 2:
            return l, pl.ds(pl.multiple_of(block * DB + half * (DB // 2), 32), DB // 2), pl.ds(s * (FF // STRIPS), FF // STRIPS)
        rows = FB // 2 // STRIPS
        return l, pl.ds(pl.multiple_of(block * FB + half * (FB // 2) + s * rows, 32), rows), slice(None)

    def copy(kind, k, src, dst, device):
        return pltpu.make_async_remote_copy(src, dst, send.at[kind, k], recv.at[kind, k], device_id=device, device_id_type=MESH)

    def x_copy(k):
        m = CHUNKS[k][1]
        return copy(0, k, shards[m].at[region(CHUNKS[k], 0, r)], fulls[m].at[region(CHUNKS[k], d, r)], over_x)

    def passed(kind, k, half, device):
        part = fulls[CHUNKS[k][1]].at[region(CHUNKS[k], across, half)]
        return copy(kind, k, part, part, device)

    def y_copy(k):
        return passed(1, k, r, over_y)

    def first_copy(k):
        return passed(2, k, r, over_chip)

    def second_copy(k):
        return passed(3, k, 1 - r, over_chip)

    def own_copy(l, m):
        rows = shards[m].shape[1]
        to = fulls[m].at[l, pl.ds(pl.multiple_of(d * rows, 32), rows)]
        return pltpu.make_async_remote_copy(shards[m].at[l], to, own_send.at[l * 3 + m], own_recv.at[l * 3 + m], device_id=over_chip, device_id_type=MESH)

    greet([over_x, over_y, over_chip])
    n = len(CHUNKS)
    for k in range(n):
        x_copy(k).start()
    for l in range(LAYERS):
        for m in range(3):
            own_copy(l, m).start()

    def event(k):
        if k < n:
            x_copy(k).wait_recv()
            y_copy(k).start()
            first_copy(k).start()
        if k:
            y_copy(k - 1).wait_recv()
            second_copy(k - 1).start()

    happened = [0]

    def upto(k):
        while happened[0] <= k:
            event(happened[0])
            happened[0] += 1

    def ready(ks):
        upto(max(ks) + 1)
        for k in ks:
            first_copy(k).wait_recv()
            second_copy(k).wait_recv()

    def at_steps(index, steps):
        for step in steps:
            @pl.when(index == step)
            def _(k=happened[0]):
                event(k)
            happened[0] += 1

    def move(_, src, dst):
        dst[...] = src[...]

    for m, rows in ((0, 160), (1, 160), (2, 512)):
        wide = shards[m].shape[2]
        pipe(move, (LAYERS, 2), [pl.BlockSpec((1, rows, wide), lambda l, i: (l, i, 0))],
             [pl.BlockSpec((1, rows, wide), lambda l, i: (l, d * 2 + i, 0))], shards[m], fulls[m])

    def prepare(at, x_ref, dy_ref, at_ref, dyt_ref):
        wide = x_ref[...].astype(F32)
        new = (wide * inverse(wide)).astype(BF16)
        a[pl.ds(at[0] * 256, 256), :] = new
        at_ref[...] = new.T
        dyt_ref[...] = dy_ref[...].T

    row, column = pl.BlockSpec((256, D), lambda i: (i, 0)), pl.BlockSpec((D, 256), lambda i: (0, i))
    pipe(prepare, (TOKENS // 256,), [row, row], [column, column], x, dy, a0_t, dy_t)

    def ffn(l, gate, up, mid, base, steps):
        for s in range(STRIPS):
            ready([base + 2 * s, base + 2 * s + 1])
            if s == 0:
                for m in (0, 1):
                    own_copy(l, m).wait_recv()
            cuts = FF // STRIPS // TN

            def body(at, wg_ref, wu_ref, gate_ref, up_ref, mid_ref):
                f, i = at
                at_steps(f * (TOKENS // TM) + i, steps)
                left = a[pl.ds(i * TM, TM), :]
                gate_ref[...] = dot(left, wg_ref[...])
                up_ref[...] = dot(left, wu_ref[...])
                g = gate_ref[...]
                mid_ref[...] = (jax.nn.sigmoid(g) * g * up_ref[...]).astype(BF16)

            before = happened[0]
            weight = pl.BlockSpec((D, TN), lambda f, i: (0, s * cuts + f))
            out = pl.BlockSpec((TM, TN), lambda f, i: (i, s * cuts + f))
            steps_now = steps

            def once(at, *refs, before=before):
                happened[0] = before
                body(at, *refs)

            pipe(once, (cuts, TOKENS // TM), [weight, weight], [out, out, out], fg.at[l], fu.at[l], gate, up, mid)
            happened[0] = before + len(steps_now)

    ffn(0, gate0, up0, mid0, 0, (4,))

    ready(list(range(8, 12)))
    own_copy(0, 2).wait_recv()
    before = happened[0]

    def down(at, mid_ref, w_ref):
        k, i = at
        happened[0] = before
        at_steps(k * (TOKENS // TM) + i, (3, 8, 13))
        rows = pl.ds(i * TM, TM)
        part = dot(mid_ref[...], w_ref[...])

        @pl.when(k == 0)
        def _():
            acc[rows, :] = part

        @pl.when(k > 0)
        def _():
            acc[rows, :] += part

    pipe(down, (4, TOKENS // TM), [pl.BlockSpec((TM, FF // 4), lambda k, i: (i, k)), pl.BlockSpec((FF // 4, D), lambda k, i: (k, 0))], [],
         mid0, fd.at[0])
    happened[0] = before + 3

    def next_state(at, x_ref, h_ref, at_ref):
        rows = pl.ds(at[0] * 256, 256)
        h = (x_ref[...].astype(F32) + acc[rows, :].astype(BF16).astype(F32)).astype(BF16)
        h_ref[...] = h
        wide = h.astype(F32)
        new = (wide * inverse(wide)).astype(BF16)
        a[rows, :] = new
        at_ref[...] = new.T

    pipe(next_state, (TOKENS // 256,), [row], [row, column], x, h1, a1_t)
    ffn(1, gate1, up1, mid1, 12, (0, 4))
    ready(list(range(20, 24)))
    own_copy(1, 2).wait_recv()
    for k in range(n):
        for c in (x_copy(k), y_copy(k), first_copy(k), second_copy(k)):
            c.wait_send()
    for l in range(LAYERS):
        for m in range(3):
            own_copy(l, m).wait_send()


UNITS = [(l, m, half) for l in (1, 0) for m in (2, 0, 1) for half in (0, 1)]
ROWS = ((2, DB, FF // 2), (2, DB, FF // 2), (2, D // 2, FB))


def backward_kernel(fg, fu, fd, dy, dy_t, x, h1, a0_t, a1_t, gate0, up0, mid0, gate1, up1, mid1,
                    dx, og, ou, od, dgate, dup, dh_t, theirs_g, mine_g, got_g, leaves_g, came_g, theirs_d, mine_d, got_d, leaves_d, came_d,
                    dh, acc, chip_send, chip_recv, x_send, x_recv):
    r, d, chip, core = place()
    over_x, over_chip = (r, (1 - chip) * 2 + core), (r, chip * 2 + 1 - core)
    grads, gates, ups, mids, a_t, d_t, states = (og, ou, od), (gate0, gate1), (up0, up1), (mid0, mid1), (a0_t, a1_t), (dh_t, dy_t), (x, h1)
    slots = {}
    for l, m, half in UNITS:
        kind = m == 2
        slots[l, m, half] = sum(1 for key in slots if (key[1] == 2) == kind)

    def buffers(u):
        at = slots[UNITS[u]]
        group = (theirs_d, mine_d, got_d, leaves_d, came_d) if UNITS[u][1] == 2 else (theirs_g, mine_g, got_g, leaves_g, came_g)
        return [ref.at[at] for ref in group]

    def chip_copy(u):
        theirs, _, got, _, _ = buffers(u)
        return pltpu.make_async_remote_copy(theirs, got, chip_send.at[u], chip_recv.at[u], device_id=over_chip, device_id_type=MESH)

    def x_copy(u):
        _, _, _, leaves, came = buffers(u)
        return pltpu.make_async_remote_copy(leaves, came, x_send.at[u], x_recv.at[u], device_id=over_x, device_id_type=MESH)

    def term(u):
        l, m, half = UNITS[u]
        theirs, mine, *_ = buffers(u)
        if m == 2:
            def body(at, left, to_send, to_keep, theirs_ref, mine_ref):
                theirs_ref[0] = dot(left[...], to_send[...]).astype(BF16)
                mine_ref[0] = dot(left[...], to_keep[...]).astype(BF16)

            cuts = FB // TN
            out = pl.BlockSpec((1, D // 2, TN), lambda j, t: (j, 0, t))
            pipe(body, (2, cuts), [
                pl.BlockSpec((D // 2, TOKENS), lambda j, t: (half, 0)),
                pl.BlockSpec((TOKENS, TN), lambda j, t: (0, (j * 2 + 1 - core) * cuts + t)),
                pl.BlockSpec((TOKENS, TN), lambda j, t: (0, (j * 2 + core) * cuts + t)),
            ], [out, out], d_t[l], mids[l], mids[l], theirs, mine)
        else:
            def body(at, left, right, theirs_ref, mine_ref):
                for j in range(2):
                    for ref, who in ((theirs_ref, 1 - core), (mine_ref, core)):
                        rows = pl.ds(pl.multiple_of((j * 2 + who) * DB, 64), DB)
                        ref[j] = dot(left[rows, :], right[...]).astype(BF16)

            cuts = FF // 2 // TN
            out = pl.BlockSpec((2, DB, TN), lambda t: (0, 0, t))
            pipe(body, (cuts,), [pl.BlockSpec((D, TOKENS), lambda t: (0, 0)), pl.BlockSpec((TOKENS, TN), lambda t: (0, half * cuts + t))],
                 [out, out], a_t[l], (dgate, dup)[m], theirs, mine)
        chip_copy(u).start()

    def leave(u):
        chip_copy(u).wait_recv()
        _, mine, got, leaves, _ = buffers(u)
        rows, wide = ROWS[UNITS[u][1]][1] // 2, ROWS[UNITS[u][1]][2]

        def body(at, mine_ref, got_ref, out_ref):
            out_ref[...] = (mine_ref[0].astype(F32) + got_ref[0].astype(F32)).astype(BF16)

        two = pl.BlockSpec((1, rows, wide), lambda i: (1 - chip, i, 0))
        pipe(body, (2,), [two, two], [pl.BlockSpec((rows, wide), lambda i: (i, 0))], mine, got, leaves)
        x_copy(u).start()

    def finish(u):
        x_copy(u).wait_recv()
        l, m, half = UNITS[u]
        _, mine, got, _, came = buffers(u)

        def body(at, mine_ref, got_ref, came_ref, out_ref):
            total = mine_ref[0].astype(F32) + got_ref[0].astype(F32) + came_ref[...].astype(F32)
            out_ref[...] = (total.T if m == 2 else total).astype(BF16)

        if m == 2:
            two = pl.BlockSpec((1, D // 2, 256), lambda i: (chip, 0, i))
            pipe(body, (FB // 256,), [two, two, pl.BlockSpec((D // 2, 256), lambda i: (0, i))], [pl.BlockSpec((256, D // 2), lambda i: (i, half))],
                 mine, got, came, grads[m].at[l])
        else:
            two = pl.BlockSpec((1, DB // 2, FF // 2), lambda i: (chip, i, 0))
            pipe(body, (2,), [two, two, pl.BlockSpec((DB // 2, FF // 2), lambda i: (i, 0))], [pl.BlockSpec((DB // 2, FF // 2), lambda i: (i, half))],
                 mine, got, came, grads[m].at[l])

    def by_mid(l, part):
        cuts = FF // TN // 2

        def body(at, w_ref, gate_ref, up_ref, dgate_ref, dup_ref):
            f, i = at
            by = dot(dh[pl.ds(i * TM, TM), :], w_ref[...], NT).astype(BF16).astype(F32)
            g = gate_ref[...]
            sig = jax.nn.sigmoid(g)
            dup_ref[...] = (by * (g * sig)).astype(BF16)
            dgate_ref[...] = (by * up_ref[...] * (sig * (1 + g * (1 - sig)))).astype(BF16)

        tile = pl.BlockSpec((TM, TN), lambda f, i: (i, part * cuts + f))
        pipe(body, (cuts, TOKENS // TM), [pl.BlockSpec((TN, D), lambda f, i: (part * cuts + f, 0)), tile, tile], [tile, tile],
             fd.at[l], gates[l], ups[l], dgate, dup)

    def by_a(l):
        def body(at, dg_ref, du_ref, wg_ref, wu_ref):
            k, i = at
            rows = pl.ds(i * TM, TM)
            part = dot(dg_ref[...], wg_ref[...], NT) + dot(du_ref[...], wu_ref[...], NT)

            @pl.when(k == 0)
            def _():
                acc[rows, :] = part

            @pl.when(k > 0)
            def _():
                acc[rows, :] += part

        left = pl.BlockSpec((TM, FF // 4), lambda k, i: (i, k))
        right = pl.BlockSpec((D, FF // 4), lambda k, i: (0, k))
        pipe(body, (4, TOKENS // TM), [left, left, right, right], [], dgate, dup, fg.at[l], fu.at[l])

    def by_h(l):
        def body(at, h_ref, out_ref):
            rows = pl.ds(at[0] * 256, 256)
            wide, da = h_ref[...].astype(F32), acc[rows, :]
            scale = inverse(wide)
            along = jnp.mean(da * wide, -1, keepdims=True)
            new = (dh[rows, :].astype(F32) + scale * (da - wide * (scale * scale * along))).astype(BF16)
            if l:
                dh[rows, :] = new
                out_ref[...] = new.T
            else:
                out_ref[...] = new

        row, column = pl.BlockSpec((256, D), lambda i: (i, 0)), pl.BlockSpec((D, 256), lambda i: (0, i))
        pipe(body, (TOKENS // 256,), [row], [column if l else row], states[l], dh_t if l else dx)

    greet([over_x, over_chip])
    pltpu.sync_copy(dy, dh)
    for l in (1, 0):
        u = 0 if l else 6
        if l == 0:
            by_mid(0, 0)
            by_mid(0, 1)
        term(u)
        term(u + 1)
        leave(u)
        if l:
            by_mid(1, 0)
        leave(u + 1)
        if l:
            by_mid(1, 1)
        term(u + 2)
        for v in range(u + 3, u + 6):
            term(v)
            leave(v - 1)
        by_a(l)
        leave(u + 5)
        by_h(l)
    for u in range(len(UNITS)):
        finish(u)
    for u in range(len(UNITS)):
        chip_copy(u).wait_send()
        x_copy(u).wait_send()


def shape(*dims, dtype=BF16):
    return jax.ShapeDtypeStruct(dims, dtype)


def call(kernel, outs, scratch, collective_id, flops, *args):
    anywhere = pl.BlockSpec(memory_space=pl.ANY)
    return pl.pallas_call(
        kernel, out_shape=outs, in_specs=[anywhere] * len(args), out_specs=[anywhere] * len(outs), scratch_shapes=scratch,
        compiler_params=pltpu.CompilerParams(collective_id=collective_id, has_side_effects=True, vmem_limit_bytes=60 * 2**20),
        cost_estimate=pl.CostEstimate(flops=flops, bytes_accessed=400_000_000, transcendentals=0),
    )(*args)


def body(x, dy, w_gate, w_up, w_down):
    x, dy = x[0], dy[0]
    matmul = 2 * TOKENS * D * FF
    hidden = [shape(TOKENS, FF, dtype=F32), shape(TOKENS, FF, dtype=F32), shape(TOKENS, FF)]
    dma = pltpu.SemaphoreType.DMA
    n = len(CHUNKS)
    fg, fu, fd, dy_t, a0_t, gate0, up0, mid0, h1, a1_t, gate1, up1, mid1 = call(
        forward_kernel,
        [shape(LAYERS, D, FF), shape(LAYERS, D, FF), shape(LAYERS, FF, D), shape(D, TOKENS), shape(D, TOKENS), *hidden, shape(TOKENS, D), shape(D, TOKENS), *hidden],
        [pltpu.VMEM((TOKENS, D), BF16), pltpu.VMEM((TOKENS, D), F32), dma((6,)), dma((6,)), dma((4, n)), dma((4, n))],
        0, 5 * matmul, x, dy, w_gate, w_up, w_down)
    two_g, two_d = shape(8, 2, DB, FF // 2), shape(4, 2, D // 2, FB)
    one_g, one_d = shape(8, DB, FF // 2), shape(4, D // 2, FB)
    units = len(UNITS)
    dx, og, ou, od, *_ = call(
        backward_kernel,
        [shape(TOKENS, D), shape(LAYERS, DB, FF), shape(LAYERS, DB, FF), shape(LAYERS, FB, D), shape(TOKENS, FF), shape(TOKENS, FF), shape(D, TOKENS),
         two_g, two_g, two_g, one_g, one_g, two_d, two_d, two_d, one_d, one_d],
        [pltpu.VMEM((TOKENS, D), BF16), pltpu.VMEM((TOKENS, D), F32)] + [dma((units,))] * 4,
        1, 12 * matmul, fg, fu, fd, dy, dy_t, x, h1, a0_t, a1_t, gate0, up0, mid0, gate1, up1, mid1)
    return dx[None], og, ou, od


def solution(mesh):
    own, rows = P(AXES), P(None, "dp")
    return jax.shard_map(body, mesh=mesh, in_specs=(own, own, rows, rows, rows), out_specs=(own, *[P("rep", "dp")] * 3), check_vma=False)
```

time: 1490 us -> 807 us (0.54)
  Pallas kernels: 0 us -> 779 us
  waiting for transfers between devices: 762 us -> 0 us
  matrix products: 519 us -> 0 us
  other arithmetic: 136 us -> 0.01 us
  local copies, waits for them, and re-layouts: 53.4 us -> 15.1 us
    pallas_call x0 -> x2, Pallas kernels: none -> 779 us  [call(): pl.pallas_call(kernel, out_shape=outs, in_specs=[anywhere] * len(args), o...]
    unnamed x18 -> x0, waiting for transfers between devices: 552 us -> none
    dot_general x17 -> x0, matrix products: 519 us -> none  [the longest x6 198 us: layer(): up = jnp.dot(a, w['w_up'], preferred_element_type=jnp.float32)]
    squeeze x6 -> x0, waiting for transfers between devices: 210 us -> none  [stack(): h = layer(h, {name: w[number] for name, w in weights.items()})]
    unnamed x3 -> x1, other arithmetic: 81.8 us -> 0.01 us
    unnamed x21 -> x12, local copies, waits for them, and re-layouts: 37.2 us -> 15.1 us
    reshape x4 -> x0, other arithmetic: 20.5 us -> none  [the longest x1 12.4 us: step(): by_x.reshape(shape)]
    broadcast_in_dim x6 -> x0, other arithmetic: 16.9 us -> none  [stack(): h = layer(h, {name: w[number] for name, w in weights.items()})]
  transfers between devices with their start and end apart: 12 -> 0, of which waited for: 10 -> 0; matrix products, arithmetic and copies ran while one was open for 35% -> 0% of each run, Pallas kernels for 0% -> 0%
where the time goes in v1:
time: 807 us; the launch traced here: 795 us
  Pallas kernels  779 us (97%)
  local copies, waits for them, and re-layouts  15.1 us (2%)
    pallas_call x2, Pallas kernels, call(): pl.pallas_call(kernel, out_shape=outs, in_specs=[anywhere] * len(args), o...  779 us

profile of v1, /device:TPU:0, one launch (start us, length us, event | category | flops | bytes accessed | tf_op | source)
XLA Modules:
  0.0 794.9 jit_solution(16688214764456911258)
XLA Ops:
  0.6 257.8 %shard_map.84 = (bf16[2,1280,4096]{2,1,0:T(8,128)(2,1)}, bf16[2,1280,4096]{2,1,0:T(8,128)(2,1)}, bf16[2,4096,1280]{2,1,0:T(8,128)(2,1)}, bf16[1280,2048]{1,0:T(8...) custom-call(bf16[2048,1280]{1,0:T(8,128)(2,1)} %bitcast.6, ...), custom_call_target="tpu_custom_call" | custom-call | flops 107374182400 | bytes 400000000 | tf_op jit(solution)/shard_map/pallas_call | solution.py:388
  258.5 520.8 %shard_map.85 = (bf16[2048,1280]{1,0:T(8,128)(2,1)}, bf16[2,320,4096]{2,1,0:T(8,128)(2,1)}, bf16[2,320,4096]{2,1,0:T(8,128)(2,1)}, bf16[2,1024,1280]{2,1,0:T(8,1...) custom-call(bf16[2,1280,4096]{2,1,0:T(8,128)(2,1)} %get-tuple-elemen, ...), custom_call_target="tpu_custom_call" | custom-call | flops 257698037760 | bytes 400000000 | tf_op jit(solution)/shard_map/pallas_call | solution.py:388
  779.3 0.0 copy-start.1
  779.3 5.3 copy.13
  784.7 0.0 copy-done.1
  784.7 0.0 copy-start
  784.7 0.0 slice-start
  784.7 2.7 copy.14
  787.3 1.7 copy-done
  789.0 0.0 slice-start.1
  789.0 2.4 copy.15
  791.5 0.0 slice-done
  791.5 0.6 slice-done.1
  792.1 2.4 copy.16
  (1 shorter events, 0.0 us)
Async XLA Ops:
  779.3 5.3 copy-start.1
  784.7 4.4 copy-start
  784.7 6.8 slice-start
  789.0 3.1 slice-start.1

commit v2 on v0

v2 whole, which is shorter than its diff:
```python
import jax
import jax.numpy as jnp
from jax import lax
from jax.experimental import pallas as pl
from jax.experimental.pallas import tpu as pltpu
from jax.sharding import PartitionSpec as P

F32, BF16 = jnp.float32, jnp.bfloat16
AXES = ("rep", "dp")
TOKENS, D, FF, LAYERS = 2048, 1280, 4096, 2
DB, FB = D // 4, FF // 4
NN, NT = (((1,), (0,)), ((), ())), (((1,), (1,)), ((), ()))
MESH = pl.DeviceIdType.MESH
TM, TN = 1024, 512


def dot(a, b, dims=NN):
    return lax.dot_general(a, b, dims, preferred_element_type=F32)


def pipe(body, grid, ins, outs, *refs):
    def step(at, *blocks):
        body(at.index, *blocks)

    pltpu.emit_pipeline(step, grid=grid, in_specs=ins, out_specs=outs, trace_scopes=False, _explicit_indices=True)(*refs)


def place():
    r, d = lax.axis_index("rep"), lax.axis_index("dp")
    return r, d, d // 2, d % 2


def named(name, f, *args):
    with jax.named_scope(name):
        return f(*args)


def greet(devices):
    barrier = pltpu.get_barrier_semaphore()
    for device in devices:
        pl.semaphore_signal(barrier, inc=1, device_id=device, device_id_type=MESH)
    pl.semaphore_wait(barrier, len(devices))


def inverse(wide):
    return lax.rsqrt(jnp.mean(wide * wide, -1, keepdims=True) + 1e-6)


STRIPS = 4
WIDE = FF // STRIPS
CHUNKS = [(0, m, s) for s in range(STRIPS) for m in (0, 1)] + [(l, 2, s) for l in (0, 1) for s in range(STRIPS)]
CHUNKS += [(1, m, s) for s in range(STRIPS) for m in (0, 1)]


def kernel(x, dy, wg, wu, wd,
           fg, fu, fd, a0_t, a1_t, silu0, slope0, mids, h1, dgu, dx,
           out_g, got_g, leaves_g, came_g, stay_g, kept_g, out_d, got_d, leaves_d, came_d, stay_d, kept_d,
           a, dh, left_a, left_d, own_send, own_recv, send, recv, w_sem, chip_send, chip_recv, x_send, x_recv):
    r, d, chip, core = place()
    across, beside = (1 - chip) * 2 + core, chip * 2 + 1 - core
    over_x, over_y, over_chip = (r, across), (1 - r, d), (r, beside)
    shards, fulls = (wg, wu, wd), (fg, fu, fd)


    def region(chunk, block, half, first):
        l, m, s = chunk
        if m < 2:
            column = pl.multiple_of(((first * 2 + s) % 4) * WIDE, WIDE)
            return l, pl.ds(pl.multiple_of(block * DB + half * (DB // 2), 32), DB // 2), pl.ds(column, WIDE)
        rows = FB // 2 // STRIPS
        return l, pl.ds(pl.multiple_of(block * FB + half * (FB // 2) + s * rows, 32), rows), slice(None)

    def copy(kind, k, src, dst, device):
        return pltpu.make_async_remote_copy(src, dst, send.at[kind, k], recv.at[kind, k], device_id=device, device_id_type=MESH)

    def x_copy(k):
        m = CHUNKS[k][1]
        return copy(0, k, shards[m].at[region(CHUNKS[k], 0, r, chip)], fulls[m].at[region(CHUNKS[k], d, r, chip)], over_x)

    def passed(kind, k, half, device):
        part = fulls[CHUNKS[k][1]].at[region(CHUNKS[k], across, half, 1 - chip)]
        return copy(kind, k, part, part, device)

    def y_copy(k):
        return passed(1, k, r, over_y)

    def first_copy(k):
        return passed(2, k, r, over_chip)

    def second_copy(k):
        return passed(3, k, 1 - r, over_chip)

    def own_copy(l, m):
        rows = shards[m].shape[1]
        to = fulls[m].at[l, pl.ds(pl.multiple_of(d * rows, 32), rows)]
        return pltpu.make_async_remote_copy(shards[m].at[l], to, own_send.at[l * 3 + m], own_recv.at[l * 3 + m], device_id=over_chip, device_id_type=MESH)

    greet([over_x, over_y, over_chip])
    n = len(CHUNKS)
    for k in range(n):
        x_copy(k).start()
    for l in range(LAYERS):
        for m in range(3):
            own_copy(l, m).start()

    def pass_on(k):
        x_copy(k).wait_recv()
        y_copy(k).start()
        first_copy(k).start()

    def share(k):
        y_copy(k).wait_recv()
        second_copy(k).start()

    LAG = 2
    passed_on, shared = [0], [0]

    def due():
        k, first = passed_on[0], shared[0]
        passed_on[0] += 1
        shared[0] = max(first, passed_on[0] - LAG)
        return k, range(first, shared[0])

    def event(k, ks):
        pass_on(k)
        for other in ks:
            share(other)

    def upto(k):
        while passed_on[0] <= k:
            event(*due())

    def ready(ks):
        upto(max(ks))
        while shared[0] <= max(ks):
            share(shared[0])
            shared[0] += 1
        for k in ks:
            first_copy(k).wait_recv()
            second_copy(k).wait_recv()

    def eventful(name, body, grid, steps, *rest):
        plan = [(step, due()) for step in steps]

        def once(at, *refs):
            now = at[0] if len(grid) == 1 else at[0] * grid[1] + at[1]
            for step, what in plan:
                @pl.when(now == step)
                def _():
                    event(*what)
            body(at, *refs)

        named(name, pipe, once, grid, *rest)

    def move(_, src, dst):
        dst[...] = src[...]

    def place_own(l, m):
        rows, wide = shards[m].shape[1] // 2, shards[m].shape[2]
        named(f"move_{l}_{m}", pipe, move, (2,), [pl.BlockSpec((rows, wide), lambda i: (i, 0))], [pl.BlockSpec((rows, wide), lambda i: (d * 2 + i, 0))],
              shards[m].at[l], fulls[m].at[l])

    def prepare(at, x_ref, dy_ref, at_ref):
        rows = pl.ds(at[0] * 256, 256)
        wide = x_ref[...].astype(F32)
        new = (wide * inverse(wide)).astype(BF16)
        a[rows, :] = new
        at_ref[...] = new.T
        dh[rows, :] = dy_ref[...]
        left_d[:, rows] = dy_ref[...].T

    row, column = pl.BlockSpec((256, D), lambda i: (i, 0)), pl.BlockSpec((D, 256), lambda i: (0, i))
    named("prepare", pipe, prepare, (TOKENS // 256,), [row, row], [column], x, dy, a0_t)
    upto(0)
    place_own(0, 0)
    upto(1)
    place_own(0, 1)
    upto(2)

    def up_front(at, wg_ref, wu_ref, silu_ref, slope_ref, mid_ref):
        left = a[pl.ds(at[1] * TM, TM), :]
        g, u = dot(left, wg_ref[...]), dot(left, wu_ref[...])
        sig = jax.nn.sigmoid(g)
        silu = g * sig
        silu_ref[...] = silu
        slope_ref[...] = u * (sig + silu * (1 - sig))
        mid_ref[...] = (silu * u).astype(BF16)

    def last(at, wg_ref, wu_ref, wd_ref, mid_ref, dgate_ref, dup_ref):
        rows = pl.ds(at[1] * TM, TM)
        left = a[rows, :]
        g, u = dot(left, wg_ref[...]), dot(left, wu_ref[...])
        by = dot(dh[rows, :], wd_ref[...], NT).astype(BF16).astype(F32)
        sig = jax.nn.sigmoid(g)
        silu = g * sig
        mid_ref[...] = (silu * u).astype(BF16)
        dup_ref[...] = (by * silu).astype(BF16)
        dgate_ref[...] = (by * (u * (sig + silu * (1 - sig)))).astype(BF16)

    cuts = WIDE // TN

    def ffn(l, s, base, steps):
        named(f"ready_{l}_{s}", ready, [base + 2 * s, base + 2 * s + 1])
        if s == 0:
            for m in (0, 1):
                own_copy(l, m).wait_recv()
        at = ((1 - chip) * 2 + s) % 4 * cuts
        weight = pl.BlockSpec((D, TN), lambda f, i: (0, at + f))
        out = pl.BlockSpec((TM, TN), lambda f, i: (i, at + f))
        if l:
            eventful(f"ffn_{l}_{s}", last, (cuts, TOKENS // TM), steps, [weight, weight, pl.BlockSpec((TN, D), lambda f, i: (at + f, 0))],
                     [out, out, out], fg.at[l], fu.at[l], fd.at[l], mids.at[l], dgu.at[l, 0], dgu.at[l, 1])
        else:
            eventful(f"ffn_{l}_{s}", up_front, (cuts, TOKENS // TM), steps, [weight, weight], [out, out, out],
                     fg.at[l], fu.at[l], silu0, slope0, mids.at[l])

    for s, steps in enumerate(((1, 3), (0, 2), (0, 2), (0, 1, 3))):
        ffn(0, s, 0, steps)

    def down(w):
        pltpu.sync_copy(fd.at[0], w)

        def body(at, mid_ref, x_ref, h_ref, at_ref):
            rows = pl.ds(at[0] * 256, 256)
            h = (x_ref[...].astype(F32) + dot(mid_ref[...], w[...]).astype(BF16).astype(F32)).astype(BF16)
            h_ref[...] = h
            wide = h.astype(F32)
            new = (wide * inverse(wide)).astype(BF16)
            a[rows, :] = new
            left_a[:, rows] = new.T
            at_ref[...] = new.T

        eventful("down", body, (TOKENS // 256,), (2, 4, 6, 7), [pl.BlockSpec((256, FF), lambda i: (i, 0)), row], [row, column], mids.at[0], x, h1, a1_t)

    place_own(0, 2)
    upto(12)
    place_own(1, 0)
    place_own(1, 1)
    named("ready_down", ready, list(range(8, 12)))
    own_copy(0, 2).wait_recv()
    upto(13)
    pl.run_scoped(down, pltpu.VMEM((FF, D), BF16))
    place_own(1, 2)


    def buffers(l, m, leaving):
        if m == 2:
            return [ref.at[l] for ref in ((out_d, got_d) if leaving else (stay_d, kept_d))]
        return [ref.at[l, m] for ref in ((out_g, got_g) if leaving else (stay_g, kept_g))]

    def chip_copy(l, m, leaving):
        term, got = buffers(l, m, leaving)
        k = (l * 3 + m) * 2 + leaving
        return pltpu.make_async_remote_copy(term.at[1 - core], got, chip_send.at[k], chip_recv.at[k], device_id=over_chip, device_id_type=MESH)

    def over(l, m):
        return (leaves_d.at[l], came_d.at[l]) if m == 2 else (leaves_g.at[l, m], came_g.at[l, m])

    def cross(l, m):
        k = l * 3 + m
        return pltpu.make_async_remote_copy(*over(l, m), x_send.at[k], x_recv.at[k], device_id=over_x, device_id_type=MESH)

    def term_down(l, leaving):
        side = 1 - chip if leaving else chip
        to = buffers(l, 2, leaving)[0]

        def body(at, right, out_ref):
            out_ref[...] = dot(left_d[...], right[...]).astype(BF16)

        cuts = FB // TN
        if leaving:
            for first, who in ((True, 1 - core), (False, core)):
                block = (side * 2 + who) * cuts
                pipe(body, (cuts,), [pl.BlockSpec((TOKENS, TN), lambda t: (0, block + t))], [pl.BlockSpec((D, TN), lambda t: (0, t))], mids.at[l], to.at[who])
                if first:
                    chip_copy(l, 2, leaving).start()
        else:
            def both(at, right, out_ref):
                body(at, right, out_ref.at[0])

            pipe(both, (2, cuts), [pl.BlockSpec((TOKENS, TN), lambda w, t: (0, (side * 2 + w) * cuts + t))], [pl.BlockSpec((1, D, TN), lambda w, t: (w, 0, t))],
                 mids.at[l], to)
            chip_copy(l, 2, leaving).start()

    def term(l, leaving, ms):
        side = 1 - chip if leaving else chip
        to = (out_g if leaving else stay_g).at[l]
        base = ms[0]

        def body(at, right, out_ref):
            rows = pl.ds(pl.multiple_of(side * (2 * DB), 128), 2 * DB)
            both = dot(left_a[rows, :], right[0]).astype(BF16)
            out_ref[0, 0] = both[:DB]
            out_ref[0, 1] = both[DB:]

        pipe(body, (len(ms), FF // TN), [pl.BlockSpec((1, TOKENS, TN), lambda m, t: (base + m, 0, t))],
             [pl.BlockSpec((1, 2, DB, TN), lambda m, t: (base + m, 0, 0, t))], dgu.at[l], to)
        for m in ms:
            chip_copy(l, m, leaving).start()

    def leave(l, m):
        named("chip_wait", chip_copy(l, m, 1).wait_recv)
        term, got = buffers(l, m, 1)

        def body(at, mine_ref, got_ref, out_ref):
            out_ref[...] = (mine_ref[...].astype(F32) + got_ref[...].astype(F32)).astype(BF16)

        spec = pl.BlockSpec((D // 4, FB) if m == 2 else (DB // 4, FF), lambda i: (i, 0))
        pipe(body, (4,), [spec, spec], [spec], term.at[core], got, over(l, m)[0])
        cross(l, m).start()

    def leave_pair(l):
        for m in (0, 1):
            chip_copy(l, m, 1).wait_recv()

        def body(at, mine_ref, got_ref, out_ref):
            out_ref[0] = (mine_ref[0, 0].astype(F32) + got_ref[0].astype(F32)).astype(BF16)

        spec = pl.BlockSpec((1, DB // 4, FF), lambda m, i: (m, i, 0))
        pipe(body, (2, 4), [pl.BlockSpec((1, 1, DB // 4, FF), lambda m, i: (m, core, i, 0)), spec], [spec], out_g.at[l], got_g.at[l], leaves_g.at[l])
        for m in (0, 1):
            cross(l, m).start()

    def by_mid(l):
        rows = 1024

        def body(at, w_ref, silu_ref, slope_ref, dgate_ref, dup_ref):
            for c in range(rows // 256):
                part = slice(c * 256, c * 256 + 256)
                by = dot(dh[pl.ds(at[1] * rows + c * 256, 256), :], w_ref[...], NT).astype(BF16).astype(F32)
                dup_ref[part, :] = (by * silu_ref[part, :]).astype(BF16)
                dgate_ref[part, :] = (by * slope_ref[part, :]).astype(BF16)

        tile = pl.BlockSpec((rows, TN), lambda f, i: (i, f))
        pipe(body, (FF // TN, TOKENS // rows), [pl.BlockSpec((TN, D), lambda f, i: (f, 0)), tile, tile], [tile, tile],
             fd.at[l], silu0, slope0, dgu.at[l, 0], dgu.at[l, 1])

    def by_a(l, meanwhile):
        def scoped(g_w, u_w):
            copies = [pltpu.make_async_copy(full.at[l], w, w_sem.at[k]) for k, (full, w) in enumerate(((fg, g_w), (fu, u_w)))]
            for c in copies:
                c.start()
            meanwhile()
            for c in copies:
                c.wait()

            def body(at, dg_ref, du_ref, h_ref, *out_ref):
                rows = pl.ds(at[0] * 256, 256)
                da = dot(dg_ref[...], g_w[...], NT) + dot(du_ref[...], u_w[...], NT)
                wide = h_ref[...].astype(F32)
                scale = inverse(wide)
                along = jnp.mean(da * wide, -1, keepdims=True)
                new = (dh[rows, :].astype(F32) + scale * (da - wide * (scale * scale * along))).astype(BF16)
                if l:
                    dh[rows, :] = new
                    left_d[:, rows] = new.T
                else:
                    out_ref[0][...] = new

            tile = pl.BlockSpec((256, FF), lambda i: (i, 0))
            named(f"by_a_{l}", pipe, body, (TOKENS // 256,), [tile, tile, row], [] if l else [row], dgu.at[l, 0], dgu.at[l, 1], h1 if l else x, *([] if l else [dx]))

        pl.run_scoped(scoped, pltpu.VMEM((D, FF), BF16), pltpu.VMEM((D, FF), BF16))

    def do(what, *args):
        named("_".join([what.__name__, *[str(v).replace(" ", "") for v in args]]), what, *args)

    named("ready_last", ready, list(range(12, 16)))
    own_copy(1, 2).wait_recv()
    ffn(1, 0, 16, (0, 0, 2, 3))
    ffn(1, 1, 16, (1, 2))
    do(term_down, 1, 1)
    do(leave, 1, 2)
    ffn(1, 2, 16, ())
    ffn(1, 3, 16, ())
    do(term, 1, 1, (0,))
    do(term, 1, 1, (1,))
    do(leave, 1, 0)
    do(leave, 1, 1)
    reload = pltpu.make_async_copy(a0_t, left_a, w_sem.at[2])
    reload.start()
    by_a(1, lambda: do(term_down, 1, 0))
    do(term_down, 0, 1)
    do(leave, 0, 2)
    do(by_mid, 0)
    reload.wait()
    do(term, 0, 1, (0, 1))
    do(term_down, 0, 0)
    do(leave_pair, 0)
    do(term, 0, 0, (0, 1))
    pltpu.sync_copy(a1_t, left_a)
    by_a(0, lambda: do(term, 1, 0, (0, 1)))
    with jax.named_scope("end"):
        for k in range(n):
            for c in (x_copy(k), y_copy(k), first_copy(k), second_copy(k)):
                c.wait_send()
        for l in range(LAYERS):
            for m in range(3):
                own_copy(l, m).wait_send()
                for leaving in (0, 1):
                    chip_copy(l, m, leaving).wait_send()
                chip_copy(l, m, 0).wait_recv()
                cross(l, m).wait()


def total(a, b, c):
    return a.astype(F32) + b.astype(F32) + c.astype(F32)


def finish_kernel(core, stay_g, kept_g, came_g, stay_u, kept_u, came_u, stay_d, kept_d, came_d, dx, og, ou, od, dx_out):
    og[0] = total(stay_g[0, 0, 0], kept_g[0, 0], came_g[0, 0]).astype(BF16)
    ou[0] = total(stay_u[0, 0, 0], kept_u[0, 0], came_u[0, 0]).astype(BF16)
    od[0] = total(stay_d[0, 0], kept_d[0], came_d[0]).astype(BF16).T
    dx_out[...] = dx[...]


def shape(*dims, dtype=BF16):
    return jax.ShapeDtypeStruct(dims, dtype)


def finish(core, stay_g, kept_g, came_g, stay_d, kept_d, came_d, dx):
    steps = 4
    rows, columns, tokens = DB // steps, FB // steps, TOKENS // (LAYERS * steps)
    ins = []
    for m in (0, 1):
        one = pl.BlockSpec((1, 1, rows, FF), lambda l, i, core, m=m: (l, m, i, 0))
        ins += [pl.BlockSpec((1, 1, 1, rows, FF), lambda l, i, core, m=m: (l, m, core[0], i, 0)), one, one]
    one = pl.BlockSpec((1, D, columns), lambda l, i, core: (l, 0, i))
    ins += [pl.BlockSpec((1, 1, D, columns), lambda l, i, core: (l, core[0], 0, i)), one, one]
    some = pl.BlockSpec((tokens, D), lambda l, i, core: (l * steps + i, 0))
    out = pl.BlockSpec((1, rows, FF), lambda l, i, core: (l, i, 0))
    return pl.pallas_call(
        finish_kernel, out_shape=[shape(LAYERS, DB, FF), shape(LAYERS, DB, FF), shape(LAYERS, FB, D), shape(TOKENS, D)],
        compiler_params=pltpu.CompilerParams(vmem_limit_bytes=60 * 2**20),
        grid_spec=pltpu.PrefetchScalarGridSpec(
            num_scalar_prefetch=1, grid=(LAYERS, steps), in_specs=[*ins, some],
            out_specs=[out, out, pl.BlockSpec((1, columns, D), lambda l, i, core: (l, i, 0)), some]),
    )(core, stay_g, kept_g, came_g, stay_g, kept_g, came_g, stay_d, kept_d, came_d, dx)


def body(x, dy, w_gate, w_up, w_down):
    x, dy = x[0], dy[0]
    dma, vmem = pltpu.SemaphoreType.DMA, pltpu.VMEM
    hidden, two_g, one_g, two_d, one_d = shape(LAYERS, TOKENS, FF), shape(LAYERS, 2, 2, DB, FF), shape(LAYERS, 2, DB, FF), shape(LAYERS, 2, D, FB), shape(LAYERS, D, FB)
    outs = dict(
        fg=shape(LAYERS, D, FF), fu=shape(LAYERS, D, FF), fd=shape(LAYERS, FF, D), a0_t=shape(D, TOKENS), a1_t=shape(D, TOKENS),
        silu0=shape(TOKENS, FF, dtype=F32), slope0=shape(TOKENS, FF, dtype=F32), mids=hidden, h1=shape(TOKENS, D), dgu=shape(LAYERS, 2, TOKENS, FF), dx=shape(TOKENS, D),
        out_g=two_g, got_g=one_g, leaves_g=one_g, came_g=one_g, stay_g=two_g, kept_g=one_g,
        out_d=two_d, got_d=one_d, leaves_d=one_d, came_d=one_d, stay_d=two_d, kept_d=one_d)
    n = len(CHUNKS)
    anywhere = pl.BlockSpec(memory_space=pl.ANY)
    done = pl.pallas_call(
        kernel, out_shape=list(outs.values()), in_specs=[anywhere] * 5, out_specs=[anywhere] * len(outs),
        scratch_shapes=[vmem((TOKENS, D), BF16), vmem((TOKENS, D), BF16), vmem((D, TOKENS), BF16), vmem((D, TOKENS), BF16), dma((6,)), dma((6,)), dma((4, n)), dma((4, n)),
                        dma((3,)), dma((12,)), dma((12,)), dma((6,)), dma((6,))],
        compiler_params=pltpu.CompilerParams(collective_id=0, has_side_effects=True, vmem_limit_bytes=60 * 2**20),
        cost_estimate=pl.CostEstimate(flops=17 * 2 * TOKENS * D * FF, bytes_accessed=800_000_000, transcendentals=0),
    )(x, dy, w_gate, w_up, w_down)
    done = dict(zip(outs, done))
    core = (lax.axis_index("dp") % 2).reshape(1).astype(jnp.int32)
    og, ou, od, dx = finish(core, *(done[k] for k in ("stay_g", "kept_g", "came_g", "stay_d", "kept_d", "came_d", "dx")))
    return dx[None], og, ou, od


def solution(mesh):
    own, rows = P(AXES), P(None, "dp")
    return jax.shard_map(body, mesh=mesh, in_specs=(own, own, rows, rows, rows), out_specs=(own, *[P("rep", "dp")] * 3), check_vma=False)
```

time: 1490 us -> 665 us (0.45)
  waiting for transfers between devices: 762 us -> 0 us
  Pallas kernels: 0 us -> 652 us
  matrix products: 519 us -> 0 us
  other arithmetic: 136 us -> 0 us
  local copies, waits for them, and re-layouts: 53.4 us -> 0 us
    pallas_call x0 -> x2, Pallas kernels: none -> 652 us  [the longest x1 628 us: body(): pl.pallas_call(kernel, out_shape=list(outs.values()), in_specs=[anywhere]...]
    unnamed x18 -> x0, waiting for transfers between devices: 552 us -> none
    dot_general x17 -> x0, matrix products: 519 us -> none  [the longest x6 198 us: layer(): up = jnp.dot(a, w['w_up'], preferred_element_type=jnp.float32)]
    squeeze x6 -> x0, waiting for transfers between devices: 210 us -> none  [stack(): h = layer(h, {name: w[number] for name, w in weights.items()})]
    unnamed x3 -> x0, other arithmetic: 81.8 us -> none
    unnamed x21 -> x0, local copies, waits for them, and re-layouts: 37.2 us -> none
    reshape x4 -> x0, other arithmetic: 20.5 us -> none  [the longest x1 12.4 us: step(): by_x.reshape(shape)]
    broadcast_in_dim x6 -> x0, other arithmetic: 16.9 us -> none  [stack(): h = layer(h, {name: w[number] for name, w in weights.items()})]
  transfers between devices with their start and end apart: 12 -> 0, of which waited for: 10 -> 0; matrix products, arithmetic and copies ran while one was open for 35% -> 0% of each run, Pallas kernels for 0% -> 0%
where the time goes in v2:
time: 665 us; the launch traced here: 654 us
  Pallas kernels  652 us (98%)
    pallas_call x1, Pallas kernels, body(): pl.pallas_call(kernel, out_shape=list(outs.values()), in_specs=[anywhere]...  628 us
    pallas_call x1, Pallas kernels, finish(): pl.pallas_call(finish_kernel, out_shape=[shape(LAYERS, DB, FF), shape(LAY...  24.9 us

profile of v2, /device:TPU:0, one launch (start us, length us, event | category | flops | bytes accessed | tf_op | source)
XLA Modules:
  0.0 653.5 jit_solution(1071516082725741192)
XLA Ops:
  0.6 627.5 %shard_map.84 = (bf16[2,1280,4096]{2,1,0:T(8,128)(2,1)}, bf16[2,1280,4096]{2,1,0:T(8,128)(2,1)}, bf16[2,4096,1280]{2,1,0:T(8,128)(2,1)}, bf16[1280,2048]{1,0:T(8...) custom-call(bf16[2048,1280]{1,0:T(8,128)(2,1)} %bitcast.4, ...), custom_call_target="tpu_custom_call" | custom-call | flops 365072220160 | bytes 800000000 | tf_op jit(solution)/shard_map/pallas_call | solution.py:452
  628.2 24.9 %shard_map.85 = (bf16[2,320,4096]{2,1,0:T(8,128)(2,1)}, bf16[2,320,4096]{2,1,0:T(8,128)(2,1)}, bf16[2,1024,1280]{2,1,0:T(8,128)(2,1)}, bf16[2048,1280]{1,0:T(8,128)(2,1)}) custom-call(s32[1]{0:T(128)} %bitcast.core, bf16[2,2,2,320,4096]{4,3,2,1,0:T(8,128)(2,1)} %get-tuple-element.15.stay_g.stay_u, bf16[2,2,320,4096]{3,2,1,0:T(8,128)(2,1)} %get-tuple-element.16.kept_g.kept_u, ...), custom_call_target="tpu_custom_call" | custom-call | tf_op jit(solution)/shard_map/pallas_call | solution.py:432

commit v3 on v2

--- a/solution.py
+++ b/solution.py
@@ -170,12 +170,12 @@
         left_d[:, rows] = dy_ref[...].T
 
     row, column = pl.BlockSpec((256, D), lambda i: (i, 0)), pl.BlockSpec((D, 256), lambda i: (0, i))
-    named("prepare", pipe, prepare, (TOKENS // 256,), [row, row], [column], x, dy, a0_t)
-    upto(0)
     place_own(0, 0)
-    upto(1)
     place_own(0, 1)
+    eventful("prepare", prepare, (TOKENS // 256,), (1, 7), [row, row], [column], x, dy, a0_t)
+    place_own(0, 2)
     upto(2)
+    place_own(1, 0)
 
     def up_front(at, wg_ref, wu_ref, silu_ref, slope_ref, mid_ref):
         left = a[pl.ds(at[1] * TM, TM), :]
@@ -214,7 +214,7 @@
             eventful(f"ffn_{l}_{s}", up_front, (cuts, TOKENS // TM), steps, [weight, weight], [out, out, out],
                      fg.at[l], fu.at[l], silu0, slope0, mids.at[l])
 
-    for s, steps in enumerate(((1, 3), (0, 2), (0, 2), (0, 1, 3))):
+    for s, steps in enumerate(((1, 3), (0, 2), (0, 2), (0, 1, 2))):
         ffn(0, s, 0, steps)
 
     def down(w):
@@ -230,11 +230,9 @@
             left_a[:, rows] = new.T
             at_ref[...] = new.T
 
-        eventful("down", body, (TOKENS // 256,), (2, 4, 6, 7), [pl.BlockSpec((256, FF), lambda i: (i, 0)), row], [row, column], mids.at[0], x, h1, a1_t)
-
-    place_own(0, 2)
+        eventful("down", body, (TOKENS // 256,), (0, 2, 4, 6), [pl.BlockSpec((256, FF), lambda i: (i, 0)), row], [row, column], mids.at[0], x, h1, a1_t)
+
     upto(12)
-    place_own(1, 0)
     place_own(1, 1)
     named("ready_down", ready, list(range(8, 12)))
     own_copy(0, 2).wait_recv()
@@ -260,7 +258,7 @@
         k = l * 3 + m
         return pltpu.make_async_remote_copy(*over(l, m), x_send.at[k], x_recv.at[k], device_id=over_x, device_id_type=MESH)
 
-    def term_down(l, leaving):
+    def term_down(l, leaving, hook=None):
         side = 1 - chip if leaving else chip
         to = buffers(l, 2, leaving)[0]
 
@@ -276,18 +274,22 @@
                     chip_copy(l, 2, leaving).start()
         else:
             def both(at, right, out_ref):
+                if hook:
+                    hook(at[0] * cuts + at[1], 2 * cuts)
                 body(at, right, out_ref.at[0])
 
             pipe(both, (2, cuts), [pl.BlockSpec((TOKENS, TN), lambda w, t: (0, (side * 2 + w) * cuts + t))], [pl.BlockSpec((1, D, TN), lambda w, t: (w, 0, t))],
                  mids.at[l], to)
             chip_copy(l, 2, leaving).start()
 
-    def term(l, leaving, ms):
+    def term(l, leaving, ms, hook=None):
         side = 1 - chip if leaving else chip
         to = (out_g if leaving else stay_g).at[l]
         base = ms[0]
 
         def body(at, right, out_ref):
+            if hook:
+                hook(at[0] * (FF // TN) + at[1], len(ms) * (FF // TN))
             rows = pl.ds(pl.multiple_of(side * (2 * DB), 128), 2 * DB)
             both = dot(left_a[rows, :], right[0]).astype(BF16)
             out_ref[0, 0] = both[:DB]
@@ -308,18 +310,6 @@
         spec = pl.BlockSpec((D // 4, FB) if m == 2 else (DB // 4, FF), lambda i: (i, 0))
         pipe(body, (4,), [spec, spec], [spec], term.at[core], got, over(l, m)[0])
         cross(l, m).start()
-
-    def leave_pair(l):
-        for m in (0, 1):
-            chip_copy(l, m, 1).wait_recv()
-
-        def body(at, mine_ref, got_ref, out_ref):
-            out_ref[0] = (mine_ref[0, 0].astype(F32) + got_ref[0].astype(F32)).astype(BF16)
-
-        spec = pl.BlockSpec((1, DB // 4, FF), lambda m, i: (m, i, 0))
-        pipe(body, (2, 4), [pl.BlockSpec((1, 1, DB // 4, FF), lambda m, i: (m, core, i, 0)), spec], [spec], out_g.at[l], got_g.at[l], leaves_g.at[l])
-        for m in (0, 1):
-            cross(l, m).start()
 
     def by_mid(l):
         rows = 1024
@@ -337,10 +327,17 @@
 
     def by_a(l, meanwhile):
         def scoped(g_w, u_w):
-            copies = [pltpu.make_async_copy(full.at[l], w, w_sem.at[k]) for k, (full, w) in enumerate(((fg, g_w), (fu, u_w)))]
-            for c in copies:
-                c.start()
-            meanwhile()
+            parts = [(full.at[l, pl.ds(k * 160, 160)], w.at[pl.ds(k * 160, 160)]) for full, w in ((fg, g_w), (fu, u_w)) for k in range(D // 160)]
+            copies = [pltpu.make_async_copy(*part, w_sem.at[k]) for k, part in enumerate(parts)]
+
+            def hook(now, steps):
+                for step in range(steps):
+                    @pl.when(now == step)
+                    def _():
+                        for c in copies[step * len(copies) // steps:(step + 1) * len(copies) // steps]:
+                            c.start()
+
+            meanwhile(hook)
             for c in copies:
                 c.wait()
 
@@ -367,7 +364,7 @@
 
     named("ready_last", ready, list(range(12, 16)))
     own_copy(1, 2).wait_recv()
-    ffn(1, 0, 16, (0, 0, 2, 3))
+    ffn(1, 0, 16, (0, 1, 2, 3))
     ffn(1, 1, 16, (1, 2))
     do(term_down, 1, 1)
     do(leave, 1, 2)
@@ -377,19 +374,23 @@
     do(term, 1, 1, (1,))
     do(leave, 1, 0)
     do(leave, 1, 1)
-    reload = pltpu.make_async_copy(a0_t, left_a, w_sem.at[2])
+    reload = pltpu.make_async_copy(a0_t, left_a, w_sem.at[16])
     reload.start()
-    by_a(1, lambda: do(term_down, 1, 0))
+    by_a(1, lambda hook: named("term_down_1_0", term_down, 1, 0, hook))
     do(term_down, 0, 1)
     do(leave, 0, 2)
     do(by_mid, 0)
     reload.wait()
-    do(term, 0, 1, (0, 1))
+    do(term, 0, 1, (0,))
+    do(term, 0, 1, (1,))
+    do(leave, 0, 0)
+    do(leave, 0, 1)
+    do(term, 0, 0, (0, 1))
+    reload = pltpu.make_async_copy(a1_t, left_a, w_sem.at[16])
+    reload.start()
     do(term_down, 0, 0)
-    do(leave_pair, 0)
-    do(term, 0, 0, (0, 1))
-    pltpu.sync_copy(a1_t, left_a)
-    by_a(0, lambda: do(term, 1, 0, (0, 1)))
+    reload.wait()
+    by_a(0, lambda hook: named("term_1_0", term, 1, 0, (0, 1), hook))
     with jax.named_scope("end"):
         for k in range(n):
             for c in (x_copy(k), y_copy(k), first_copy(k), second_copy(k)):
@@ -452,7 +453,7 @@
     done = pl.pallas_call(
         kernel, out_shape=list(outs.values()), in_specs=[anywhere] * 5, out_specs=[anywhere] * len(outs),
         scratch_shapes=[vmem((TOKENS, D), BF16), vmem((TOKENS, D), BF16), vmem((D, TOKENS), BF16), vmem((D, TOKENS), BF16), dma((6,)), dma((6,)), dma((4, n)), dma((4, n)),
-                        dma((3,)), dma((12,)), dma((12,)), dma((6,)), dma((6,))],
+                        dma((17,)), dma((12,)), dma((12,)), dma((6,)), dma((6,))],
         compiler_params=pltpu.CompilerParams(collective_id=0, has_side_effects=True, vmem_limit_bytes=60 * 2**20),
         cost_estimate=pl.CostEstimate(flops=17 * 2 * TOKENS * D * FF, bytes_accessed=800_000_000, transcendentals=0),
     )(x, dy, w_gate, w_up, w_down)

time: 665 us -> 653 us (0.982)
  Pallas kernels: 652 us -> 640 us
    pallas_call x1, Pallas kernels: 628 us -> 615 us  [body(): pl.pallas_call(kernel, out_shape=list(outs.values()), in_specs=[anywhere]...]
where the time goes in v3:
time: 653 us; the launch traced here: 641 us
  Pallas kernels  640 us (98%)
    pallas_call x1, Pallas kernels, body(): pl.pallas_call(kernel, out_shape=list(outs.values()), in_specs=[anywhere]...  615 us
    pallas_call x1, Pallas kernels, finish(): pl.pallas_call(finish_kernel, out_shape=[shape(LAYERS, DB, FF), shape(LAY...  24.9 us

profile of v3, /device:TPU:0, one launch (start us, length us, event | category | flops | bytes accessed | tf_op | source)
XLA Modules:
  0.0 641.4 jit_solution(7203596286110373579)
XLA Ops:
  0.6 615.3 %shard_map.84 = (bf16[2,1280,4096]{2,1,0:T(8,128)(2,1)}, bf16[2,1280,4096]{2,1,0:T(8,128)(2,1)}, bf16[2,4096,1280]{2,1,0:T(8,128)(2,1)}, bf16[1280,2048]{1,0:T(8...) custom-call(bf16[2048,1280]{1,0:T(8,128)(2,1)} %bitcast.4, ...), custom_call_target="tpu_custom_call" | custom-call | flops 365072220160 | bytes 800000000 | tf_op jit(solution)/shard_map/pallas_call | solution.py:453
  616.0 24.9 %shard_map.85 = (bf16[2,320,4096]{2,1,0:T(8,128)(2,1)}, bf16[2,320,4096]{2,1,0:T(8,128)(2,1)}, bf16[2,1024,1280]{2,1,0:T(8,128)(2,1)}, bf16[2048,1280]{1,0:T(8,128)(2,1)}) custom-call(s32[1]{0:T(128)} %bitcast.core, bf16[2,2,2,320,4096]{4,3,2,1,0:T(8,128)(2,1)} %get-tuple-element.15.stay_g.stay_u, bf16[2,2,320,4096]{3,2,1,0:T(8,128)(2,1)} %get-tuple-element.16.kept_g.kept_u, ...), custom_call_target="tpu_custom_call" | custom-call | tf_op jit(solution)/shard_map/pallas_call | solution.py:433
